TPU v7x, 32 devices: a whole 2x2x4 slice. The times are simulated.
32 devices in a mesh: dp: 32 (over z, y, x, core), tensor: 1.
Axes of the slice: x: 2, y: 2, z: 4, core: 2. Of those that a mesh axis runs over, the one named last changes fastest.
Arguments:
- grad_codes: bfloat16 [4, 32, 32, 18432], P(None, 'dp', None, 'tensor'), may hold values from -448 to 448
- exponents: int32 [4, 32, 16], P(None, 'dp'), may hold values from 7 to 10
- accumulated: bfloat16 [32, 18432], P('dp', 'tensor'), may hold values from -12 to 12
- arrival: int32 [32], replicated, may hold values from 0 to 31, each once
- bucket_of_row: int32 [32], replicated, may hold values from 0 to 15, never falling along the last dimension, each value on 1 to 4 neighbouring positions
Outputs:
- unit_codes: bfloat16 [4, 32, 18432], P(None, 'dp', 'tensor')
- bucket_peaks: float32 [4, 16], replicated
- compensated: float32 [32, 18432], P('dp', 'tensor')
Inputs may be any that keep to these rules, and one draw needn't show every extreme that they name: `arrival`: each weight row appears in exactly one slot. `bucket_of_row`: bucket numbers never fall along the rows; each bucket holds 1 to 4 consecutive rows and one holds exactly 4.
All inputs are finite; a program needn't handle non-finite values.
Results may differ from a plain program's by a relative error of at most 0.001.
Values sent between devices are 32-bit elements; how exact they have to be, the bound alone decides.
A program may use at most 64 MiB of HBM per device.

v0:
```python
import functools

import jax
import jax.numpy as jnp
from jax import lax
from jax.experimental import pallas as pl
from jax.experimental.pallas import tpu as pltpu
from jax.sharding import PartitionSpec as P

epsilon = 1e-06
LANES = 128


def bit_orders(bits):
    head = list(range(1, min(4, bits)))
    tail = list(range(1 + len(head), bits))
    return [[0] + head[r:] + head[:r] + tail for r in range(max(1, len(head)))]


def chunks_of(tiles, count):
    plans = {18: PLAN}
    plan = plans.get(tiles, [(1,) * count] * (tiles // count)) if count == 3 else [(tiles,) + (0,) * (count - 1)]
    plan = [list(row) for row in plan]
    plan[0][0] += tiles - sum(map(sum, plan))
    spans, at = [], 0
    for row in plan:
        spans.append([])
        for wide in row:
            spans[-1].append((at * LANES, wide * LANES))
            at += wide
    return spans


PLAN = [(2, 1, 1), (2, 2, 1), (2, 2, 1), (2, 1, 1)]


def exchange(n, orders, spans, codes, exponents, accumulated, arrival, bucket_of_row, exact, peak_table, own_peak, x, lhs,
             begin, out, acc, peak, table, x_sem, send_sem, recv_sem, peak_send, peak_recv, *lands):
    me = lax.axis_index("dp")
    bits = n.bit_length() - 1
    steps, size, width = x.shape
    rows = codes.shape[2]
    groups = size // rows
    half = rows // 2
    loads = []
    for c, row in enumerate(spans):
        first, wide = row[0][0], sum(w for _, w in row)
        loads.append([])
        for g in range(groups):
            copy = pltpu.make_async_copy(
                codes.at[:, 0, :, pl.ds(g * width + first, wide)],
                x.at[:, pl.ds(g * rows, rows), pl.ds(first, wide)],
                x_sem.at[c, g],
            )
            copy.start()
            loads[-1].append(copy)

    barrier = pltpu.get_barrier_semaphore()

    def greet(j, carry):
        pl.semaphore_signal(barrier, inc=1, device_id={"dp": lax.rem(me + j, n)}, device_id_type=pl.DeviceIdType.MESH)
        return carry

    lax.fori_loop(1, n, greet, 0)

    partners = []
    for b in range(bits):
        stride = 1 << b
        bit = lax.rem(me // stride, 2)
        partners.append(me + stride * (1 - 2 * bit))

    slot = lax.broadcasted_iota(jnp.int32, (1, size), 1) % rows
    held = jnp.zeros((1, size), jnp.int32)
    scale = [jnp.zeros((1, size), jnp.int32) for _ in range(steps)]
    for k in range(rows):
        row = arrival[k]
        bucket = bucket_of_row[row]
        here = slot == k
        held = jnp.where(here, row, held)
        for s in range(steps):
            scale[s] = jnp.where(here, exponents[s, 0, bucket], scale[s])
    scale = [jnp.exp2(-e.astype(jnp.float32)) for e in scale]

    row_group = lax.broadcasted_iota(jnp.int32, (size, 1), 0) % groups
    col_group = lax.broadcasted_iota(jnp.int32, (1, size), 1) // rows
    wanted = held * groups + col_group
    place = lax.broadcasted_iota(jnp.int32, (size, 1), 0) // groups
    for q, order in enumerate(orders):
        owner = jnp.zeros_like(place)
        for m, b in enumerate(order):
            bit = (place // (1 << (bits - 1 - m))) % 2
            mine = lax.rem(me // (1 << b), 2)
            owner = owner + ((bit + mine) % 2) * (1 << b)
        mask = owner * groups + row_group == wanted
        for s in range(steps):
            lhs[q, s] = jnp.where(mask, scale[s], 0.0).astype(jnp.bfloat16)
    for g in range(groups):
        begin[g : g + 1, :] = accumulated[:, g * width : (g + 1) * width].astype(jnp.float32)

    def copy_of(c, q, k):
        at, wide = spans[c][q]
        count = half >> k
        cols = pl.ds(at, wide)
        source = out.at[:, :, :, cols] if k == 0 else acc.at[:, pl.ds(count, count), :, cols]
        return pltpu.make_async_remote_copy(
            src_ref=source,
            dst_ref=lands[k].at[:, :, :, cols],
            send_sem=send_sem.at[c, q, k],
            recv_sem=recv_sem.at[c, q, k],
            device_id={"dp": partners[orders[q][k]]},
            device_id_type=pl.DeviceIdType.MESH,
        )

    def stage(c, q, k):
        at, wide = spans[c][q]
        cols = pl.ds(at, wide)
        if k == 0:
            split = half * groups
            for s in range(steps):
                part = jnp.dot(lhs[q, s], x[s, :, cols], preferred_element_type=jnp.float32)
                out[s, :, :, cols] = part[split:].reshape(half, groups, wide)
                acc[s, :, :, cols] = part[:split].reshape(half, groups, wide)
            if c == 0 and q == 0:
                pl.semaphore_wait(barrier, n - 1)
            copy_of(c, q, 0).start()
            return
        copy_of(c, q, k - 1).wait_recv()
        count = half >> k
        got = lands[k - 1]
        if k < bits:
            acc[:, count : 2 * count, :, cols] += got[:, count : 2 * count, :, cols]
            copy_of(c, q, k).start()
            acc[:, 0:count, :, cols] += got[:, 0:count, :, cols]
        else:
            acc[:, 0:1, :, cols] += got[:, 0:1, :, cols]

    tops = [jnp.zeros((groups, 1), jnp.float32) for _ in range(steps)]
    for wave in range(len(spans) + bits):
        for k in range(bits + 1):
            c = wave - k
            if c < 0 or c >= len(spans):
                continue
            streams = [q for q in range(len(orders)) if spans[c][q][1]]
            if k == 0:
                for copy in loads[c]:
                    copy.wait()
            for q in streams:
                stage(c, q, k)
            if k == bits:
                first, wide = spans[c][0][0], sum(w for _, w in spans[c])
                running = begin[:, first : first + wide]
                carried = jnp.zeros_like(running)
                for s in range(steps):
                    adjusted = acc[s, 0, :, first : first + wide] - carried
                    new = (running + adjusted).astype(jnp.bfloat16).astype(jnp.float32)
                    carried = (new - running) - adjusted
                    running = new
                    total = new - carried
                    tops[s] = jnp.maximum(tops[s], jnp.max(jnp.abs(total), axis=1, keepdims=True))
                    for g in range(groups):
                        exact[s : s + 1, g * width + first : g * width + first + wide] = total[g : g + 1, :]

    lane = lax.broadcasted_iota(jnp.int32, (1, LANES), 1)
    row = jnp.zeros((1, LANES), jnp.float32)
    for s in range(steps):
        row = jnp.where(lane == s, jnp.max(tops[s], axis=0, keepdims=True), row)
    peak[...] = row

    def peak_copy(j):
        return pltpu.make_async_remote_copy(
            src_ref=peak,
            dst_ref=table.at[me],
            send_sem=peak_send.at[j],
            recv_sem=peak_recv.at[j],
            device_id={"dp": lax.rem(me + j, n)},
            device_id_type=pl.DeviceIdType.MESH,
        )

    def tell(j, carry):
        peak_copy(j).start()
        return carry

    def hear(j, carry):
        peak_copy(j).wait()
        return carry

    lax.fori_loop(1, n, tell, 0)
    table[me] = row
    for c in range(len(spans)):
        for q in range(len(orders)):
            if spans[c][q][1]:
                for k in range(bits):
                    copy_of(c, q, k).wait_send()
    lax.fori_loop(1, n, hear, 0)

    buckets = exponents.shape[2]
    by_bucket = jnp.zeros((buckets, LANES), jnp.float32)
    own = jnp.zeros((1, LANES), jnp.float32)
    bucket_id = lax.broadcasted_iota(jnp.int32, (buckets, LANES), 0)
    lane_id = lax.broadcasted_iota(jnp.int32, (buckets, LANES), 1)
    my_bucket = bucket_of_row[me]
    for i in range(rows):
        bucket = bucket_of_row[i]
        by_bucket = jnp.maximum(by_bucket, jnp.where(bucket_id == bucket, table[i], 0.0))
    own = jnp.max(jnp.where(bucket_id == my_bucket, by_bucket, 0.0), axis=0, keepdims=True)
    for s in range(steps):
        turned = jnp.sum(jnp.where(bucket_id == lane_id, by_bucket[:, s : s + 1], 0.0), axis=0, keepdims=True)
        peak_table[s : s + 1, :] = turned[:, :buckets]
        own_peak[s : s + 1, :] = jnp.broadcast_to(own[:, s : s + 1], (1, LANES))


def on_device(n, tensor, grad_codes, exponents, accumulated, arrival, bucket_of_row):
    steps, _, rows, columns = grad_codes.shape
    buckets = exponents.shape[2]
    bits = n.bit_length() - 1
    groups = max(g for g in (1, 2, 4, 8) if columns % (g * LANES) == 0)
    width = columns // groups
    orders = bit_orders(bits)
    spans = chunks_of(width // LANES, len(orders))
    half = rows // 2
    vmem = pl.BlockSpec(memory_space=pltpu.VMEM)
    smem = pl.BlockSpec(memory_space=pltpu.SMEM)
    exact, peak_table, own_peaks = pl.pallas_call(
        functools.partial(exchange, n, orders, spans),
        out_shape=(
            jax.ShapeDtypeStruct((steps, columns), jnp.float32),
            jax.ShapeDtypeStruct((steps, buckets), jnp.float32),
            jax.ShapeDtypeStruct((steps, LANES), jnp.float32),
        ),
        in_specs=[pl.BlockSpec(memory_space=pl.ANY), smem, vmem, smem, smem],
        out_specs=(vmem, vmem, vmem),
        scratch_shapes=[
            pltpu.VMEM((steps, groups * rows, width), jnp.bfloat16),
            pltpu.VMEM((len(orders), steps, groups * rows, groups * rows), jnp.bfloat16),
            pltpu.VMEM((groups, width), jnp.float32),
            pltpu.VMEM((steps, half, groups, width), jnp.float32),
            pltpu.VMEM((steps, half, groups, width), jnp.float32),
            pltpu.VMEM((1, LANES), jnp.float32),
            pltpu.VMEM((n, 1, LANES), jnp.float32),
            pltpu.SemaphoreType.DMA((len(spans), groups)),
            pltpu.SemaphoreType.DMA((len(spans), len(orders), bits)),
            pltpu.SemaphoreType.DMA((len(spans), len(orders), bits)),
            pltpu.SemaphoreType.DMA((n,)),
            pltpu.SemaphoreType.DMA((n,)),
        ]
        + [pltpu.VMEM((steps, half >> k, groups, width), jnp.float32) for k in range(bits)],
        compiler_params=pltpu.CompilerParams(
            collective_id=0, has_side_effects=True, vmem_limit_bytes=56 * 1024 * 1024
        ),
    )(grad_codes, exponents, accumulated, arrival, bucket_of_row)

    own_peaks = own_peaks[:, :1]
    if tensor > 1:
        peak_table = lax.pmax(peak_table, "tensor")
        own = lax.dynamic_slice_in_dim(bucket_of_row, lax.axis_index("dp"), 1, 0)
        own_member = own[:, None] == jnp.arange(buckets, dtype=jnp.int32)[None, :]
        own_peaks = jnp.max(jnp.where(own_member, peak_table, 0.0), axis=1, keepdims=True)
    unit = (exact / (own_peaks + epsilon)).astype(jnp.bfloat16)
    return unit.reshape(steps, 1, columns), peak_table, exact[steps - 1 :]


def solution(mesh):
    return jax.shard_map(
        functools.partial(on_device, mesh.shape["dp"], mesh.shape["tensor"]),
        mesh=mesh,
        in_specs=(P(None, "dp", None, "tensor"), P(None, "dp", None), P("dp", "tensor"), P(), P()),
        out_specs=(P(None, "dp", "tensor"), P(), P("dp", "tensor")),
        check_vma=False,
    )
```

profile of v0, /device:TPU:0, one launch (start us, length us, event | category | flops | bytes accessed | tf_op | source)
XLA Modules:
  0.0 64.7 jit_solution(2631162927087867603)
XLA Ops:
  0.6 58.6 %shard_map.76 = (f32[4,18432]{1,0:T(4,128)}, f32[4,16]{1,0:T(4,128)}, f32[4,128]{1,0:T(4,128)}) custom-call(bf16[4,1,32,18432]{3,2,1,0:T(8,128)(2,1)} %codes.1, s32[4,1,16]{2,1,0:T(1,128)} %exponents.1, bf16[1,18432]{1,0:T(2,128)(2,1)} %accumulated.1, s32[32]{0:T(128)} %arrival.1, s32[32]{0:T(128)} %bucket_of_row.1), custom_call_target="tpu_custom_call" | custom-call | tf_op jit(solution)/shard_map/pallas_call | solution.py:223
  59.3 0.8 %add_reduce_fusion = f32[4]{0:T(128)S(1)} fusion(f32[4,128]{1,0:T(4,128)} %get-tuple-element.7), kind=kLoop, calls=%fused_computation.2 | loop fusion | flops 4 | bytes 32 | tf_op jit(solution)/shard_map/add | solution.py:258
  60.1 1.7 %fusion = bf16[4,1,18432]{2,0,1:T(4,128)(2,1)} fusion(f32[4,18432]{1,0:T(4,128)} %get-tuple-element.6, f32[4]{0:T(128)S(1)} %add_reduce_fusion), kind=kLoop, calls=%fused_computation.1 | loop fusion | flops 147456 | bytes 442384 | tf_op jit(solution)/shard_map/reshape | solution.py:259
  61.8 1.7 %slice.7 = f32[1,18432]{1,0:T(1,128)} slice(f32[4,18432]{1,0:T(4,128)} %get-tuple-element.6), slice={[3:4], [0:18432]} | slice | bytes 147456 | tf_op jit(solution)/shard_map/slice | solution.py:259
  63.5 1.3 %copy.9 = f32[4,16]{1,0:T(4,128)} copy(f32[4,16]{1,0:T(4,128)} %get-tuple-element.13) | data formatting | bytes 512
where the time goes:
time: 65 us; the launch traced here: 64.7 us
  Pallas kernels  58.6 us (90%)
  local copies, waits for them, and re-layouts  2.93 us (5%)
  other arithmetic  2.54 us (4%)
    pallas_call x1, Pallas kernels, on_device(): pl.pallas_call(functools.partial(exchange, n, orders, spans), out_shape=(...  58.6 us
    reshape x1, other arithmetic, on_device(): return (unit.reshape(steps, 1, columns), peak_table, exact[steps - 1:])  1.75 us
    slice x1, local copies, waits for them, and re-layouts, on_device(): return (unit.reshape(steps, 1, columns), peak_table, exact[steps - 1:])  1.67 us

commit v1 on v0

--- a/solution.py
+++ b/solution.py
@@ -9,6 +9,7 @@
 
 epsilon = 1e-06
 LANES = 128
+VMEM_LIMIT = 48 * 1024 * 1024
 
 
 def bit_orders(bits):
@@ -34,14 +35,22 @@
 PLAN = [(2, 1, 1), (2, 2, 1), (2, 2, 1), (2, 1, 1)]
 
 
-def exchange(n, orders, spans, codes, exponents, accumulated, arrival, bucket_of_row, exact, peak_table, own_peak, x, lhs,
-             begin, out, acc, peak, table, x_sem, send_sem, recv_sem, peak_send, peak_recv, *lands):
+def exchange(n, orders, spans, codes, exponents_in, accumulated_in, arrival_in, bucket_in, exact, peaks, exponents, accumulated,
+             arrival, bucket_of_row, small_sem, x, lhs, begin, out, acc, peak, table, x_sem, send_sem, recv_sem, peak_send, peak_recv, *lands):
     me = lax.axis_index("dp")
     bits = n.bit_length() - 1
     steps, size, width = x.shape
     rows = codes.shape[2]
     groups = size // rows
     half = rows // 2
+    small = [
+        pltpu.make_async_copy(source, target, small_sem.at[k])
+        for k, (source, target) in enumerate(
+            [(exponents_in, exponents), (arrival_in, arrival), (bucket_in, bucket_of_row), (accumulated_in, accumulated)]
+        )
+    ]
+    for copy in small:
+        copy.start()
     loads = []
     for c, row in enumerate(spans):
         first, wide = row[0][0], sum(w for _, w in row)
@@ -57,18 +66,16 @@
 
     barrier = pltpu.get_barrier_semaphore()
 
-    def greet(j, carry):
-        pl.semaphore_signal(barrier, inc=1, device_id={"dp": lax.rem(me + j, n)}, device_id_type=pl.DeviceIdType.MESH)
-        return carry
-
-    lax.fori_loop(1, n, greet, 0)
-
     partners = []
     for b in range(bits):
         stride = 1 << b
         bit = lax.rem(me // stride, 2)
         partners.append(me + stride * (1 - 2 * bit))
-
+    for partner in partners:
+        pl.semaphore_signal(barrier, inc=1, device_id={"dp": partner}, device_id_type=pl.DeviceIdType.MESH)
+
+    for copy in small:
+        copy.wait()
     slot = lax.broadcasted_iota(jnp.int32, (1, size), 1) % rows
     held = jnp.zeros((1, size), jnp.int32)
     scale = [jnp.zeros((1, size), jnp.int32) for _ in range(steps)]
@@ -121,7 +128,7 @@
                 out[s, :, :, cols] = part[split:].reshape(half, groups, wide)
                 acc[s, :, :, cols] = part[:split].reshape(half, groups, wide)
             if c == 0 and q == 0:
-                pl.semaphore_wait(barrier, n - 1)
+                pl.semaphore_wait(barrier, bits)
             copy_of(c, q, 0).start()
             return
         copy_of(c, q, k - 1).wait_recv()
@@ -193,20 +200,28 @@
                     copy_of(c, q, k).wait_send()
     lax.fori_loop(1, n, hear, 0)
 
-    buckets = exponents.shape[2]
-    by_bucket = jnp.zeros((buckets, LANES), jnp.float32)
-    own = jnp.zeros((1, LANES), jnp.float32)
+    for i in range(n):
+        peaks[i : i + 1, :] = table[i]
+
+
+def finish(exact, peaks, bucket_of_row, unit, peak_table, last):
+    steps = exact.shape[0]
+    buckets = peak_table.shape[1]
     bucket_id = lax.broadcasted_iota(jnp.int32, (buckets, LANES), 0)
     lane_id = lax.broadcasted_iota(jnp.int32, (buckets, LANES), 1)
-    my_bucket = bucket_of_row[me]
-    for i in range(rows):
-        bucket = bucket_of_row[i]
-        by_bucket = jnp.maximum(by_bucket, jnp.where(bucket_id == bucket, table[i], 0.0))
-    own = jnp.max(jnp.where(bucket_id == my_bucket, by_bucket, 0.0), axis=0, keepdims=True)
+    by_bucket = jnp.zeros((buckets, LANES), jnp.float32)
+    for i in range(peaks.shape[0]):
+        by_bucket = jnp.maximum(by_bucket, jnp.where(bucket_id == bucket_of_row[i], peaks[i : i + 1, :], 0.0))
+    mine = bucket_of_row[lax.axis_index("dp")]
+    own = jnp.max(jnp.where(bucket_id == mine, by_bucket, 0.0), axis=0, keepdims=True)
     for s in range(steps):
         turned = jnp.sum(jnp.where(bucket_id == lane_id, by_bucket[:, s : s + 1], 0.0), axis=0, keepdims=True)
         peak_table[s : s + 1, :] = turned[:, :buckets]
-        own_peak[s : s + 1, :] = jnp.broadcast_to(own[:, s : s + 1], (1, LANES))
+    step_id = lax.broadcasted_iota(jnp.int32, (steps, LANES), 0)
+    lane_id = lax.broadcasted_iota(jnp.int32, (steps, LANES), 1)
+    scale = jnp.sum(jnp.where(step_id == lane_id, own, 0.0), axis=1, keepdims=True) + epsilon
+    unit[...] = (exact[...] / scale).astype(jnp.bfloat16)
+    last[...] = exact[steps - 1 :, :]
 
 
 def on_device(n, tensor, grad_codes, exponents, accumulated, arrival, bucket_of_row):
@@ -220,16 +235,21 @@
     half = rows // 2
     vmem = pl.BlockSpec(memory_space=pltpu.VMEM)
     smem = pl.BlockSpec(memory_space=pltpu.SMEM)
-    exact, peak_table, own_peaks = pl.pallas_call(
+    operands = (grad_codes, exponents, accumulated, arrival, bucket_of_row)
+    exact, peaks = pl.pallas_call(
         functools.partial(exchange, n, orders, spans),
         out_shape=(
             jax.ShapeDtypeStruct((steps, columns), jnp.float32),
-            jax.ShapeDtypeStruct((steps, buckets), jnp.float32),
-            jax.ShapeDtypeStruct((steps, LANES), jnp.float32),
+            jax.ShapeDtypeStruct((n, LANES), jnp.float32),
         ),
-        in_specs=[pl.BlockSpec(memory_space=pl.ANY), smem, vmem, smem, smem],
-        out_specs=(vmem, vmem, vmem),
+        in_specs=[pl.BlockSpec(memory_space=pltpu.HBM)] * 5,
+        out_specs=(vmem, vmem),
         scratch_shapes=[
+            pltpu.SMEM(exponents.shape, jnp.int32),
+            pltpu.VMEM(accumulated.shape, jnp.bfloat16),
+            pltpu.SMEM(arrival.shape, jnp.int32),
+            pltpu.SMEM(bucket_of_row.shape, jnp.int32),
+            pltpu.SemaphoreType.DMA((4,)),
             pltpu.VMEM((steps, groups * rows, width), jnp.bfloat16),
             pltpu.VMEM((len(orders), steps, groups * rows, groups * rows), jnp.bfloat16),
             pltpu.VMEM((groups, width), jnp.float32),
@@ -245,16 +265,30 @@
         ]
         + [pltpu.VMEM((steps, half >> k, groups, width), jnp.float32) for k in range(bits)],
         compiler_params=pltpu.CompilerParams(
-            collective_id=0, has_side_effects=True, vmem_limit_bytes=56 * 1024 * 1024
+            collective_id=0, has_side_effects=True, vmem_limit_bytes=VMEM_LIMIT
         ),
-    )(grad_codes, exponents, accumulated, arrival, bucket_of_row)
-
-    own_peaks = own_peaks[:, :1]
-    if tensor > 1:
-        peak_table = lax.pmax(peak_table, "tensor")
-        own = lax.dynamic_slice_in_dim(bucket_of_row, lax.axis_index("dp"), 1, 0)
-        own_member = own[:, None] == jnp.arange(buckets, dtype=jnp.int32)[None, :]
-        own_peaks = jnp.max(jnp.where(own_member, peak_table, 0.0), axis=1, keepdims=True)
+    )(*(pltpu.with_memory_space_constraint(a, pltpu.HBM) for a in operands))
+
+    if tensor == 1:
+        unit, peak_table, last = pl.pallas_call(
+            finish,
+            out_shape=(
+                jax.ShapeDtypeStruct((steps, columns), jnp.bfloat16),
+                jax.ShapeDtypeStruct((steps, buckets), jnp.float32),
+                jax.ShapeDtypeStruct((1, columns), jnp.float32),
+            ),
+            in_specs=[vmem, vmem, smem],
+            out_specs=(vmem, vmem, vmem),
+            compiler_params=pltpu.CompilerParams(vmem_limit_bytes=8 * 1024 * 1024),
+        )(exact, peaks, bucket_of_row)
+        return unit.reshape(steps, 1, columns), peak_table, last
+
+    member = bucket_of_row[:, None] == jnp.arange(buckets, dtype=jnp.int32)[None, :]
+    by_bucket = jnp.max(jnp.where(member[:, :, None], peaks[:, None, :steps], 0.0), axis=0)
+    peak_table = lax.pmax(by_bucket.T, "tensor")
+    own = lax.dynamic_slice_in_dim(bucket_of_row, lax.axis_index("dp"), 1, 0)
+    own_member = own[:, None] == jnp.arange(buckets, dtype=jnp.int32)[None, :]
+    own_peaks = jnp.max(jnp.where(own_member, peak_table, 0.0), axis=1, keepdims=True)
     unit = (exact / (own_peaks + epsilon)).astype(jnp.bfloat16)
     return unit.reshape(steps, 1, columns), peak_table, exact[steps - 1 :]
 

time: 65 us -> 57.8 us (0.89)
  local copies, waits for them, and re-layouts: 2.93 us -> 0.01 us
  other arithmetic: 2.54 us -> 0 us
  Pallas kernels: 58.6 us -> 57 us
    pallas_call x1, Pallas kernels: 58.6 us -> 55.6 us  [on_device(): pl.pallas_call(functools.partial(exchange, n, orders, spans), out_shape=(...]
    reshape x1 -> x0, other arithmetic: 1.75 us -> none  [on_device(): return (unit.reshape(steps, 1, columns), peak_table, exact[steps - 1:])]
    slice x1 -> x0, local copies, waits for them, and re-layouts: 1.67 us -> none  [on_device(): return (unit.reshape(steps, 1, columns), peak_table, exact[steps - 1:])]
    pallas_call x0 -> x1, Pallas kernels: none -> 1.38 us  [on_device(): pl.pallas_call(finish, out_shape=(jax.ShapeDtypeStruct((steps, columns),...]
    unnamed x1 -> x2, local copies, waits for them, and re-layouts: 1.26 us -> 0.01 us
    add x1 -> x0, other arithmetic: 0.79 us -> none  [on_device(): unit = (exact / (own_peaks + epsilon)).astype(jnp.bfloat16)]
where the time goes in v1:
time: 57.8 us; the launch traced here: 57.7 us
  Pallas kernels  57 us (99%)
  between operations  0.66 us (1%)
    pallas_call x1, Pallas kernels, on_device(): pl.pallas_call(functools.partial(exchange, n, orders, spans), out_shape=(...  55.6 us
    pallas_call x1, Pallas kernels, on_device(): pl.pallas_call(finish, out_shape=(jax.ShapeDtypeStruct((steps, columns),...  1.38 us

profile of v1, /device:TPU:0, one launch (start us, length us, event | category | flops | bytes accessed | tf_op | source)
XLA Modules:
  0.0 57.7 jit_solution(5452685205094610437)
XLA Ops:
  0.6 0.0 copy-start
  0.6 55.6 %shard_map.76 = (f32[4,18432]{1,0:T(4,128)S(1)}, f32[32,128]{1,0:T(8,128)S(1)}) custom-call(bf16[4,1,32,18432]{3,2,1,0:T(8,128)(2,1)} %codes.1, s32[4,1,16]{2,1,0:T(1,128)} %exponents_in.1, bf16[1,18432]{1,0:T(2,128)(2,1)} %accumulated_in.1, s32[32]{0:T(128)} %arrival_in.1, s32[32]{0:T(128)} %bucket_of_row.1), custom_call_target="tpu_custom_call" | custom-call | tf_op jit(solution)/shard_map/pallas_call | solution.py:239
  56.3 0.0 copy-done
  56.3 1.4 %shard_map.77 = (bf16[4,18432]{1,0:T(4,128)(2,1)}, f32[4,16]{1,0:T(4,128)}, f32[1,18432]{1,0:T(1,128)}) custom-call(f32[4,18432]{1,0:T(4,128)S(1)} %get-tuple-element.8.exact, f32[32,128]{1,0:T(8,128)S(1)} %get-tuple-element.9.peaks, s32[32]{0:T(128)S(1)} %copy-done), custom_call_target="tpu_custom_call" | custom-call | tf_op jit(solution)/shard_map/pallas_call | solution.py:273
Async XLA Ops:
  0.6 55.7 %copy-start = (s32[32]{0:T(128)S(1)}, s32[32]{0:T(128)}, u32[]{:S(2)}) copy-start(s32[32]{0:T(128)} %bucket_of_row.1) | copy-start | bytes 388

commit v2 on v1

v2 whole, which is shorter than its diff:
```python
import functools

import jax
import jax.numpy as jnp
from jax import lax
from jax.experimental import pallas as pl
from jax.experimental.pallas import tpu as pltpu
from jax.sharding import PartitionSpec as P

epsilon = 1e-06
LANES = 128
VMEM_LIMIT = 48 * 1024 * 1024

ORDERS = [
    (0, 1, 2, 3, 4), (0, 2, 3, 1, 4), (0, 3, 1, 2, 4), (0, 2, 1, 3, 4),
    (0, 2, 3, 4, 1), (0, 1, 3, 4, 2), (0, 3, 4, 1, 2),
]
UNITS = [
    (0, 1, 0, 4, 6), (1, 1, 0, 4, 3), (2, 1, 0, 4, 5), (3, 1, 0, 4, 2), (4, 1, 0, 4, 1),
    (5, 1, 0, 4, 6), (6, 1, 0, 4, 0), (7, 1, 0, 4, 4), (8, 1, 0, 4, 4), (9, 1, 0, 4, 4),
    (10, 1, 0, 4, 0), (11, 1, 0, 4, 3), (12, 1, 0, 4, 3), (13, 1, 0, 4, 5), (14, 1, 0, 4, 0),
    (15, 1, 0, 4, 0), (16, 1, 0, 4, 0), (17, 1, 0, 4, 0),
]
TURNS = [
    0, 1, 2, 3, 0, 4, 5, 1, 2, 6, 5, 6, 7, 8, 9, 4, 7, 1, 2, 10, 11, 12, 13, 14,
    15, 3, 9, 5, 10, 1, 15, 8, 7, 6, 12, 4, 16, 0, 13, 10, 14, 9, 13, 8, 1, 16, 7, 12,
    11, 2, 17, 9, 10, 13, 6, 15, 17, 16, 12, 10, 8, 3, 4, 11, 14, 0, 15, 1, 16, 6, 7, 17,
    2, 12, 14, 15, 13, 3, 5, 4, 17, 16, 8, 11, 6, 9, 3, 0, 2, 14, 10, 17, 12, 16, 8, 5,
    9, 15, 11, 13, 3, 4, 14, 17, 5, 7, 0, 11,
]
CUTS = (2, 6)


def plan_of(bits, tiles, steps):
    if bits == 5 and tiles == 18 and steps == 4:
        return ORDERS, UNITS, TURNS, CUTS
    head = list(range(1, min(4, bits)))
    tail = list(range(1 + len(head), bits))
    orders = [[0] + head[r:] + head[:r] + tail for r in range(max(1, len(head)))]
    units = [(t, 1, 0, steps, t % len(orders)) for t in range(tiles)]
    turns = [w - k for w in range(tiles + bits) for k in range(bits + 1) if 0 <= w - k < tiles]
    return orders, units, turns, (1,)


def across(b):
    return (1 << b) | (b > 0)


def exchange(n, plan, codes, exponents_in, accumulated_in, arrival_in, bucket_in, exact, peaks, exponents, accumulated,
             arrival, bucket_of_row, small_sem, x, lhs, begin, out, acc, peak, table, x_sem, send_sem, recv_sem,
             peak_send, peak_recv, *lands):
    orders, units, turns, cuts = plan
    me = lax.axis_index("dp")
    bits = n.bit_length() - 1
    steps, size, width = x.shape
    rows = codes.shape[2]
    groups = size // rows
    half = rows // 2
    tiles = width // LANES

    small = [
        pltpu.make_async_copy(source, target, small_sem.at[k])
        for k, (source, target) in enumerate(
            [(arrival_in, arrival), (bucket_in, bucket_of_row), (exponents_in, exponents), (accumulated_in, accumulated)]
        )
    ]
    edges = [0, *(c for c in cuts if c < tiles), tiles]
    loads = []
    for c in range(len(edges) - 1):
        first, wide = edges[c] * LANES, (edges[c + 1] - edges[c]) * LANES
        loads.append(
            [
                pltpu.make_async_copy(
                    codes.at[:, 0, :, pl.ds(g * width + first, wide)],
                    x.at[:, pl.ds(g * rows, rows), pl.ds(first, wide)],
                    x_sem.at[c, g],
                )
                for g in range(groups)
            ]
        )
    for copy in small[:3] + loads[0]:
        copy.start()

    barrier = pltpu.get_barrier_semaphore()
    partners = []
    for b in range(bits):
        partners.append(me ^ across(b))
    for partner in partners:
        pl.semaphore_signal(barrier, inc=1, device_id={"dp": partner}, device_id_type=pl.DeviceIdType.MESH)
    for group in loads[1:]:
        for copy in group:
            copy.start()
    small[3].start()

    for copy in small[:3]:
        copy.wait()
    lane = lax.broadcasted_iota(jnp.int32, (1, size), 1)
    slot = lane & (rows - 1)
    held = jnp.zeros((1, size), jnp.int32)
    scale = [jnp.zeros((1, size), jnp.int32) for _ in range(steps)]
    for k in range(rows):
        row = arrival[k]
        bucket = bucket_of_row[row]
        here = slot == k
        held = jnp.where(here, row, held)
        for s in range(steps):
            scale[s] = jnp.where(here, exponents[s, 0, bucket], scale[s])
    scale = [jnp.exp2(-e.astype(jnp.float32)) for e in scale]
    row_shift = rows.bit_length() - 1
    group_shift = groups.bit_length() - 1
    wanted = ((held ^ me) << group_shift) + (lane >> row_shift)
    line = lax.broadcasted_iota(jnp.int32, (size, 1), 0)

    def spread(q):
        target = line & (groups - 1)
        for m, b in enumerate(orders[q]):
            target = target ^ (((line >> (bits - 1 - m + group_shift)) & 1) * (across(b) << group_shift))
        mask = target == wanted
        for s in range(steps):
            lhs[q, s] = jnp.where(mask, scale[s], 0.0).astype(jnp.bfloat16)

    def copy_of(u, k):
        at, wide, s, count, q = units[u]
        cols, which, part = pl.ds(at * LANES, wide * LANES), pl.ds(s, count), half >> k
        source = out.at[which, :, :, cols] if k == 0 else acc.at[which, pl.ds(part, part), :, cols]
        return pltpu.make_async_remote_copy(
            src_ref=source,
            dst_ref=lands[k].at[which, :, :, cols],
            send_sem=send_sem.at[k],
            recv_sem=recv_sem.at[u, k],
            device_id={"dp": partners[orders[q][k]]},
            device_id_type=pl.DeviceIdType.MESH,
        )

    built, loaded, greeted = set(), 0, False
    done = [0] * len(units)
    left = {}
    for at, wide, *_ in units:
        left[at, wide] = left.get((at, wide), 0) + 1
    tops = [jnp.zeros((groups, LANES), jnp.float32) for _ in range(steps)]
    begun = False
    for u in turns:
        at, wide, s0, count, q = units[u]
        k, done[u] = done[u], done[u] + 1
        first, last, cols = at * LANES, (at + wide) * LANES, pl.ds(at * LANES, wide * LANES)
        which = pl.ds(s0, count)
        if k == 0:
            if q not in built:
                spread(q)
                built.add(q)
            while edges[loaded] < at + wide:
                for copy in loads[loaded]:
                    copy.wait()
                loaded += 1
            split = half * groups
            for s in range(s0, s0 + count):
                product = jnp.dot(lhs[q, s], x[s, :, cols], preferred_element_type=jnp.float32)
                out[s, :, :, cols] = product[split:].reshape(half, groups, last - first)
                acc[s, :, :, cols] = product[:split].reshape(half, groups, last - first)
            if not greeted:
                pl.semaphore_wait(barrier, bits)
                greeted = True
            copy_of(u, 0).start()
            continue
        copy_of(u, k - 1).wait_recv()
        part, got = half >> k, lands[k - 1]
        if k < bits:
            acc[which, part : 2 * part, :, cols] += got[which, part : 2 * part, :, cols]
            copy_of(u, k).start()
            acc[which, 0:part, :, cols] += got[which, 0:part, :, cols]
            continue
        acc[which, 0:1, :, cols] += got[which, 0:1, :, cols]
        left[at, wide] -= 1
        if left[at, wide]:
            continue
        if not begun:
            small[3].wait()
            for g in range(groups):
                begin[g : g + 1, :] = accumulated[:, g * width : (g + 1) * width].astype(jnp.float32)
            begun = True
        running = begin[:, first:last]
        carried = jnp.zeros_like(running)
        for s in range(steps):
            adjusted = acc[s, 0, :, first:last] - carried
            new = (running + adjusted).astype(jnp.bfloat16).astype(jnp.float32)
            carried = (new - running) - adjusted
            running = new
            total = new - carried
            for t in range(wide):
                tops[s] = jnp.maximum(tops[s], jnp.abs(total[:, t * LANES : (t + 1) * LANES]))
            for g in range(groups):
                exact[s : s + 1, g * width + first : g * width + last] = total[g : g + 1, :]

    lane = lax.broadcasted_iota(jnp.int32, (1, LANES), 1)
    row = jnp.zeros((1, LANES), jnp.float32)
    for s in range(steps):
        top = jnp.max(jnp.max(tops[s], axis=0, keepdims=True), axis=1, keepdims=True)
        row = jnp.where(lane == s, top, row)
    peak[...] = row

    def everything(source, target, sent, received, device):
        return pltpu.make_async_remote_copy(
            src_ref=source,
            dst_ref=target,
            send_sem=sent,
            recv_sem=received,
            device_id={"dp": device},
            device_id_type=pl.DeviceIdType.MESH,
        )

    def peak_copy(j):
        return pltpu.make_async_remote_copy(
            src_ref=peak,
            dst_ref=table.at[me],
            send_sem=peak_send,
            recv_sem=peak_recv,
            device_id={"dp": lax.rem(me + j, n)},
            device_id_type=pl.DeviceIdType.MESH,
        )

    def tell(j, carry):
        peak_copy(j).start()
        return carry

    lax.fori_loop(1, n, tell, 0)
    table[me] = row
    for k in range(bits):
        everything(lands[k], lands[k], send_sem.at[k], recv_sem.at[0, 0], partners[0]).wait_send()
    others = everything(table.at[pl.ds(1, n - 1)], table.at[pl.ds(1, n - 1)], peak_send, peak_recv, partners[0])
    others.wait_send()
    others.wait_recv()
    for i in range(n):
        peaks[i : i + 1, :] = table[i]


def finish(exact, peaks, bucket_of_row, unit, peak_table, last):
    steps = exact.shape[0]
    buckets = peak_table.shape[1]
    bucket_id = lax.broadcasted_iota(jnp.int32, (buckets, LANES), 0)
    lane_id = lax.broadcasted_iota(jnp.int32, (buckets, LANES), 1)
    by_bucket = jnp.zeros((buckets, LANES), jnp.float32)
    for i in range(peaks.shape[0]):
        by_bucket = jnp.maximum(by_bucket, jnp.where(bucket_id == bucket_of_row[i], peaks[i : i + 1, :], 0.0))
    mine = bucket_of_row[lax.axis_index("dp")]
    own = jnp.max(jnp.where(bucket_id == mine, by_bucket, 0.0), axis=0, keepdims=True)
    for s in range(steps):
        turned = jnp.sum(jnp.where(bucket_id == lane_id, by_bucket[:, s : s + 1], 0.0), axis=0, keepdims=True)
        peak_table[s : s + 1, :] = turned[:, :buckets]
    step_id = lax.broadcasted_iota(jnp.int32, (steps, LANES), 0)
    lane_id = lax.broadcasted_iota(jnp.int32, (steps, LANES), 1)
    scale = jnp.sum(jnp.where(step_id == lane_id, own, 0.0), axis=1, keepdims=True) + epsilon
    unit[...] = (exact[...] / scale).astype(jnp.bfloat16)
    last[...] = exact[steps - 1 :, :]


def on_device(n, tensor, grad_codes, exponents, accumulated, arrival, bucket_of_row):
    steps, _, rows, columns = grad_codes.shape
    buckets = exponents.shape[2]
    bits = n.bit_length() - 1
    groups = max(g for g in (1, 2, 4, 8) if columns % (g * LANES) == 0)
    width = columns // groups
    plan = plan_of(bits, width // LANES, steps)
    orders, units, _, cuts = plan
    half = rows // 2
    vmem = pl.BlockSpec(memory_space=pltpu.VMEM)
    smem = pl.BlockSpec(memory_space=pltpu.SMEM)
    operands = (grad_codes, exponents, accumulated, arrival, bucket_of_row)
    exact, peaks = pl.pallas_call(
        functools.partial(exchange, n, plan),
        out_shape=(
            jax.ShapeDtypeStruct((steps, columns), jnp.float32),
            jax.ShapeDtypeStruct((n, LANES), jnp.float32),
        ),
        in_specs=[pl.BlockSpec(memory_space=pltpu.HBM)] * 5,
        out_specs=(vmem, vmem),
        scratch_shapes=[
            pltpu.SMEM(exponents.shape, jnp.int32),
            pltpu.VMEM(accumulated.shape, jnp.bfloat16),
            pltpu.SMEM(arrival.shape, jnp.int32),
            pltpu.SMEM(bucket_of_row.shape, jnp.int32),
            pltpu.SemaphoreType.DMA((4,)),
            pltpu.VMEM((steps, groups * rows, width), jnp.bfloat16),
            pltpu.VMEM((len(orders), steps, groups * rows, groups * rows), jnp.bfloat16),
            pltpu.VMEM((groups, width), jnp.float32),
            pltpu.VMEM((steps, half, groups, width), jnp.float32),
            pltpu.VMEM((steps, half, groups, width), jnp.float32),
            pltpu.VMEM((1, LANES), jnp.float32),
            pltpu.VMEM((n, 1, LANES), jnp.float32),
            pltpu.SemaphoreType.DMA((len(cuts) + 1, groups)),
            pltpu.SemaphoreType.DMA((bits,)),
            pltpu.SemaphoreType.DMA((len(units), bits)),
            pltpu.SemaphoreType.DMA,
            pltpu.SemaphoreType.DMA,
        ]
        + [pltpu.VMEM((steps, half >> k, groups, width), jnp.float32) for k in range(bits)],
        compiler_params=pltpu.CompilerParams(
            collective_id=0, has_side_effects=True, vmem_limit_bytes=VMEM_LIMIT
        ),
    )(*(pltpu.with_memory_space_constraint(a, pltpu.HBM) for a in operands))

    if tensor == 1:
        unit, peak_table, last = pl.pallas_call(
            finish,
            out_shape=(
                jax.ShapeDtypeStruct((steps, columns), jnp.bfloat16),
                jax.ShapeDtypeStruct((steps, buckets), jnp.float32),
                jax.ShapeDtypeStruct((1, columns), jnp.float32),
            ),
            in_specs=[vmem, vmem, smem],
            out_specs=(vmem, vmem, vmem),
            compiler_params=pltpu.CompilerParams(vmem_limit_bytes=8 * 1024 * 1024),
        )(exact, peaks, bucket_of_row)
        return unit.reshape(steps, 1, columns), peak_table, last

    member = bucket_of_row[:, None] == jnp.arange(buckets, dtype=jnp.int32)[None, :]
    by_bucket = jnp.max(jnp.where(member[:, :, None], peaks[:, None, :steps], 0.0), axis=0)
    peak_table = lax.pmax(by_bucket.T, "tensor")
    own = lax.dynamic_slice_in_dim(bucket_of_row, lax.axis_index("dp"), 1, 0)
    own_member = own[:, None] == jnp.arange(buckets, dtype=jnp.int32)[None, :]
    own_peaks = jnp.max(jnp.where(own_member, peak_table, 0.0), axis=1, keepdims=True)
    unit = (exact / (own_peaks + epsilon)).astype(jnp.bfloat16)
    return unit.reshape(steps, 1, columns), peak_table, exact[steps - 1 :]


def solution(mesh):
    return jax.shard_map(
        functools.partial(on_device, mesh.shape["dp"], mesh.shape["tensor"]),
        mesh=mesh,
        in_specs=(P(None, "dp", None, "tensor"), P(None, "dp", None), P("dp", "tensor"), P(), P()),
        out_specs=(P(None, "dp", "tensor"), P(), P("dp", "tensor")),
        check_vma=False,
    )
```

time: 57.8 us -> 53 us (0.917)
  Pallas kernels: 57 us -> 52.2 us
    pallas_call x1, Pallas kernels: 55.6 us -> 50.8 us  [on_device(): pl.pallas_call(functools.partial(exchange, n, plan), out_shape=(jax.Shape...]
where the time goes in v2:
time: 53 us; the launch traced here: 52.8 us
  Pallas kernels  52.2 us (98%)
  between operations  0.66 us (1%)
    pallas_call x1, Pallas kernels, on_device(): pl.pallas_call(functools.partial(exchange, n, plan), out_shape=(jax.Shape...  50.8 us
    pallas_call x1, Pallas kernels, on_device(): pl.pallas_call(finish, out_shape=(jax.ShapeDtypeStruct((steps, columns),...  1.38 us

profile of v2, /device:TPU:0, one launch (start us, length us, event | category | flops | bytes accessed | tf_op | source)
XLA Modules:
  0.0 52.8 jit_solution(13765148169930243235)
XLA Ops:
  0.6 0.0 copy-start
  0.6 50.8 %shard_map.76 = (f32[4,18432]{1,0:T(4,128)S(1)}, f32[32,128]{1,0:T(8,128)S(1)}) custom-call(bf16[4,1,32,18432]{3,2,1,0:T(8,128)(2,1)} %codes.1, s32[4,1,16]{2,1,0:T(1,128)} %exponents_in.1, bf16[1,18432]{1,0:T(2,128)(2,1)} %accumulated_in.1, s32[32]{0:T(128)} %arrival_in.1, s32[32]{0:T(128)} %bucket_of_row.1), custom_call_target="tpu_custom_call" | custom-call | tf_op jit(solution)/shard_map/pallas_call | solution.py:268
  51.4 0.0 copy-done
  51.4 1.4 %shard_map.77 = (bf16[4,18432]{1,0:T(4,128)(2,1)}, f32[4,16]{1,0:T(4,128)}, f32[1,18432]{1,0:T(1,128)}) custom-call(f32[4,18432]{1,0:T(4,128)S(1)} %get-tuple-element.8.exact, f32[32,128]{1,0:T(8,128)S(1)} %get-tuple-element.9.peaks, s32[32]{0:T(128)S(1)} %copy-done), custom_call_target="tpu_custom_call" | custom-call | tf_op jit(solution)/shard_map/pallas_call | solution.py:302
Async XLA Ops:
  0.6 50.8 %copy-start = (s32[32]{0:T(128)S(1)}, s32[32]{0:T(128)}, u32[]{:S(2)}) copy-start(s32[32]{0:T(128)} %bucket_of_row.1) | copy-start | bytes 388

commit v3 on v2

--- a/solution.py
+++ b/solution.py
@@ -12,21 +12,23 @@
 VMEM_LIMIT = 48 * 1024 * 1024
 
 ORDERS = [
-    (0, 1, 2, 3, 4), (0, 2, 3, 1, 4), (0, 3, 1, 2, 4), (0, 2, 1, 3, 4),
-    (0, 2, 3, 4, 1), (0, 1, 3, 4, 2), (0, 3, 4, 1, 2),
+    (0, 2, 3, 1, 4), (0, 2, 1, 3, 4), (0, 1, 3, 4, 2), (0, 3, 2, 1, 4),
+    (0, 3, 4, 2, 1),
 ]
 UNITS = [
-    (0, 1, 0, 4, 6), (1, 1, 0, 4, 3), (2, 1, 0, 4, 5), (3, 1, 0, 4, 2), (4, 1, 0, 4, 1),
-    (5, 1, 0, 4, 6), (6, 1, 0, 4, 0), (7, 1, 0, 4, 4), (8, 1, 0, 4, 4), (9, 1, 0, 4, 4),
-    (10, 1, 0, 4, 0), (11, 1, 0, 4, 3), (12, 1, 0, 4, 3), (13, 1, 0, 4, 5), (14, 1, 0, 4, 0),
-    (15, 1, 0, 4, 0), (16, 1, 0, 4, 0), (17, 1, 0, 4, 0),
+    (0, 1, 0, 2, 4), (1, 1, 0, 2, 2), (1, 1, 2, 2, 1), (2, 1, 0, 4, 2), (3, 1, 0, 4, 4),
+    (4, 1, 0, 4, 1), (0, 1, 2, 2, 2), (5, 1, 0, 4, 1), (6, 1, 0, 4, 1), (7, 1, 0, 4, 2),
+    (8, 1, 0, 4, 1), (9, 1, 0, 4, 0), (10, 1, 0, 4, 2), (11, 1, 0, 2, 3), (12, 1, 0, 2, 3),
+    (13, 1, 0, 2, 1), (14, 1, 0, 4, 1), (13, 1, 2, 2, 1), (11, 1, 2, 2, 1), (15, 1, 0, 4, 2),
+    (16, 1, 0, 4, 2), (12, 1, 2, 2, 1), (17, 1, 0, 2, 1), (17, 1, 2, 2, 1),
 ]
 TURNS = [
-    0, 1, 2, 3, 0, 4, 5, 1, 2, 6, 5, 6, 7, 8, 9, 4, 7, 1, 2, 10, 11, 12, 13, 14,
-    15, 3, 9, 5, 10, 1, 15, 8, 7, 6, 12, 4, 16, 0, 13, 10, 14, 9, 13, 8, 1, 16, 7, 12,
-    11, 2, 17, 9, 10, 13, 6, 15, 17, 16, 12, 10, 8, 3, 4, 11, 14, 0, 15, 1, 16, 6, 7, 17,
-    2, 12, 14, 15, 13, 3, 5, 4, 17, 16, 8, 11, 6, 9, 3, 0, 2, 14, 10, 17, 12, 16, 8, 5,
-    9, 15, 11, 13, 3, 4, 14, 17, 5, 7, 0, 11,
+    0, 1, 2, 3, 4, 5, 0, 1, 6, 2, 7, 8, 3, 9, 4, 5, 10, 6, 11, 7, 12, 8, 13, 9,
+    14, 0, 15, 10, 16, 1, 2, 11, 17, 18, 12, 19, 13, 14, 20, 15, 21, 16, 22, 17, 23, 18, 19, 3,
+    20, 21, 5, 22, 4, 23, 0, 1, 6, 13, 7, 9, 2, 14, 8, 4, 1, 3, 12, 6, 10, 9, 2, 19,
+    3, 11, 6, 12, 15, 20, 9, 2, 19, 5, 16, 7, 11, 12, 17, 8, 19, 18, 20, 10, 5, 15, 21, 7,
+    8, 16, 22, 11, 10, 17, 20, 23, 15, 0, 18, 5, 13, 21, 7, 16, 14, 22, 8, 17, 4, 23, 1, 11,
+    0, 3, 18, 6, 13, 10, 21, 9, 15, 12, 14, 19, 22, 20, 4, 23, 16, 17, 13, 18, 21, 14, 22, 23,
 ]
 CUTS = (2, 6)
 
@@ -42,14 +44,39 @@
     return orders, units, turns, (1,)
 
 
+def slots_of(plan, bits):
+    orders, units, turns, _ = plan
+    seen, start, wait = [0] * len(units), {}, {}
+    for at, u in enumerate(turns):
+        k, seen[u] = seen[u], seen[u] + 1
+        if k < bits:
+            start[u, k] = at
+        if k > 0:
+            wait[u, k - 1] = at
+    dim = {c: orders[units[c[0]][4]][c[1]] for c in start}
+    slots, held = {}, []
+    for c in sorted(start, key=start.get):
+        there = [v for v in start if dim[v] == dim[c] and wait[v] <= start[c]]
+        latest = max((start[v] for v in there), default=-1)
+        for slot, last in enumerate(held):
+            if wait[last] <= latest:
+                slots[c], held[slot] = slot, c
+                break
+        else:
+            slots[c] = len(held)
+            held.append(c)
+    return slots
+
+
 def across(b):
     return (1 << b) | (b > 0)
 
 
-def exchange(n, plan, codes, exponents_in, accumulated_in, arrival_in, bucket_in, exact, peaks, exponents, accumulated,
-             arrival, bucket_of_row, small_sem, x, lhs, begin, out, acc, peak, table, x_sem, send_sem, recv_sem,
+def exchange(n, plan, codes, exponents_in, accumulated_in, arrival_in, bucket_in, exact, last_row, peak_table, scales, exponents,
+             accumulated, arrival, bucket_of_row, small_sem, x, lhs, begin, out, acc, peak, table, x_sem, send_sem, recv_sem,
              peak_send, peak_recv, *lands):
     orders, units, turns, cuts = plan
+    slots = slots_of(plan, n.bit_length() - 1)
     me = lax.axis_index("dp")
     bits = n.bit_length() - 1
     steps, size, width = x.shape
@@ -73,7 +100,7 @@
                 pltpu.make_async_copy(
                     codes.at[:, 0, :, pl.ds(g * width + first, wide)],
                     x.at[:, pl.ds(g * rows, rows), pl.ds(first, wide)],
-                    x_sem.at[c, g],
+                    x_sem.at[c],
                 )
                 for g in range(groups)
             ]
@@ -111,12 +138,12 @@
     wanted = ((held ^ me) << group_shift) + (lane >> row_shift)
     line = lax.broadcasted_iota(jnp.int32, (size, 1), 0)
 
-    def spread(q):
+    def spread(q, wanted_steps):
         target = line & (groups - 1)
         for m, b in enumerate(orders[q]):
             target = target ^ (((line >> (bits - 1 - m + group_shift)) & 1) * (across(b) << group_shift))
         mask = target == wanted
-        for s in range(steps):
+        for s in wanted_steps:
             lhs[q, s] = jnp.where(mask, scale[s], 0.0).astype(jnp.bfloat16)
 
     def copy_of(u, k):
@@ -127,7 +154,7 @@
             src_ref=source,
             dst_ref=lands[k].at[which, :, :, cols],
             send_sem=send_sem.at[k],
-            recv_sem=recv_sem.at[u, k],
+            recv_sem=recv_sem.at[slots[u, k]],
             device_id={"dp": partners[orders[q][k]]},
             device_id_type=pl.DeviceIdType.MESH,
         )
@@ -145,12 +172,13 @@
         first, last, cols = at * LANES, (at + wide) * LANES, pl.ds(at * LANES, wide * LANES)
         which = pl.ds(s0, count)
         if k == 0:
-            if q not in built:
-                spread(q)
-                built.add(q)
+            missing = [s for s in range(s0, s0 + count) if (q, s) not in built]
+            if missing:
+                spread(q, missing)
+                built.update((q, s) for s in missing)
             while edges[loaded] < at + wide:
-                for copy in loads[loaded]:
-                    copy.wait()
+                chunk = x.at[:, :, pl.ds(edges[loaded] * LANES, (edges[loaded + 1] - edges[loaded]) * LANES)]
+                pltpu.make_async_copy(chunk, chunk, x_sem.at[loaded]).wait()
                 loaded += 1
             split = half * groups
             for s in range(s0, s0 + count):
@@ -190,6 +218,8 @@
                 tops[s] = jnp.maximum(tops[s], jnp.abs(total[:, t * LANES : (t + 1) * LANES]))
             for g in range(groups):
                 exact[s : s + 1, g * width + first : g * width + last] = total[g : g + 1, :]
+        for g in range(groups):
+            last_row[:, g * width + first : g * width + last] = total[g : g + 1, :]
 
     lane = lax.broadcasted_iota(jnp.int32, (1, LANES), 1)
     row = jnp.zeros((1, LANES), jnp.float32)
@@ -214,7 +244,7 @@
             dst_ref=table.at[me],
             send_sem=peak_send,
             recv_sem=peak_recv,
-            device_id={"dp": lax.rem(me + j, n)},
+            device_id={"dp": me ^ (n - j)},
             device_id_type=pl.DeviceIdType.MESH,
         )
 
@@ -225,32 +255,40 @@
     lax.fori_loop(1, n, tell, 0)
     table[me] = row
     for k in range(bits):
-        everything(lands[k], lands[k], send_sem.at[k], recv_sem.at[0, 0], partners[0]).wait_send()
+        everything(lands[k], lands[k], send_sem.at[k], recv_sem.at[0], partners[0]).wait_send()
     others = everything(table.at[pl.ds(1, n - 1)], table.at[pl.ds(1, n - 1)], peak_send, peak_recv, partners[0])
     others.wait_send()
     others.wait_recv()
-    for i in range(n):
-        peaks[i : i + 1, :] = table[i]
-
-
-def finish(exact, peaks, bucket_of_row, unit, peak_table, last):
-    steps = exact.shape[0]
-    buckets = peak_table.shape[1]
+    buckets = exponents.shape[2]
     bucket_id = lax.broadcasted_iota(jnp.int32, (buckets, LANES), 0)
     lane_id = lax.broadcasted_iota(jnp.int32, (buckets, LANES), 1)
     by_bucket = jnp.zeros((buckets, LANES), jnp.float32)
-    for i in range(peaks.shape[0]):
-        by_bucket = jnp.maximum(by_bucket, jnp.where(bucket_id == bucket_of_row[i], peaks[i : i + 1, :], 0.0))
-    mine = bucket_of_row[lax.axis_index("dp")]
-    own = jnp.max(jnp.where(bucket_id == mine, by_bucket, 0.0), axis=0, keepdims=True)
+    for i in range(n):
+        by_bucket = jnp.maximum(by_bucket, jnp.where(bucket_id == bucket_of_row[i], table[i], 0.0))
+    own = jnp.max(jnp.where(bucket_id == bucket_of_row[me], by_bucket, 0.0), axis=0, keepdims=True)
     for s in range(steps):
         turned = jnp.sum(jnp.where(bucket_id == lane_id, by_bucket[:, s : s + 1], 0.0), axis=0, keepdims=True)
         peak_table[s : s + 1, :] = turned[:, :buckets]
-    step_id = lax.broadcasted_iota(jnp.int32, (steps, LANES), 0)
-    lane_id = lax.broadcasted_iota(jnp.int32, (steps, LANES), 1)
-    scale = jnp.sum(jnp.where(step_id == lane_id, own, 0.0), axis=1, keepdims=True) + epsilon
-    unit[...] = (exact[...] / scale).astype(jnp.bfloat16)
-    last[...] = exact[steps - 1 :, :]
+        scales[s : s + 1, :] = 1.0 / (jnp.broadcast_to(own[:, s : s + 1], (1, LANES)) + epsilon)
+
+
+def finish(exact, last_row, peaks, scales, unit, peak_table, last, codes, sem):
+    columns = exact.shape[1]
+    copies = [
+        pltpu.make_async_copy(last_row, last, sem.at[0]),
+        pltpu.make_async_copy(peaks, peak_table, sem.at[1]),
+    ]
+    for copy in copies:
+        copy.start()
+    scale = scales[:, :1]
+    half = columns // 2
+    for h in range(2):
+        part = pl.ds(h * half, half)
+        codes[:, part] = (exact[:, part] * scale).astype(jnp.bfloat16)
+        copies.append(pltpu.make_async_copy(codes.at[:, part], unit.at[:, part], sem.at[2 + h]))
+        copies[-1].start()
+    for copy in copies:
+        copy.wait()
 
 
 def on_device(n, tensor, grad_codes, exponents, accumulated, arrival, bucket_of_row):
@@ -263,16 +301,17 @@
     orders, units, _, cuts = plan
     half = rows // 2
     vmem = pl.BlockSpec(memory_space=pltpu.VMEM)
-    smem = pl.BlockSpec(memory_space=pltpu.SMEM)
     operands = (grad_codes, exponents, accumulated, arrival, bucket_of_row)
-    exact, peaks = pl.pallas_call(
+    exact, last_row, peaks, scales = pl.pallas_call(
         functools.partial(exchange, n, plan),
         out_shape=(
             jax.ShapeDtypeStruct((steps, columns), jnp.float32),
-            jax.ShapeDtypeStruct((n, LANES), jnp.float32),
+            jax.ShapeDtypeStruct((1, columns), jnp.float32),
+            jax.ShapeDtypeStruct((steps, buckets), jnp.float32),
+            jax.ShapeDtypeStruct((steps, LANES), jnp.float32),
         ),
         in_specs=[pl.BlockSpec(memory_space=pltpu.HBM)] * 5,
-        out_specs=(vmem, vmem),
+        out_specs=(vmem,) * 4,
         scratch_shapes=[
             pltpu.SMEM(exponents.shape, jnp.int32),
             pltpu.VMEM(accumulated.shape, jnp.bfloat16),
@@ -286,9 +325,9 @@
             pltpu.VMEM((steps, half, groups, width), jnp.float32),
             pltpu.VMEM((1, LANES), jnp.float32),
             pltpu.VMEM((n, 1, LANES), jnp.float32),
-            pltpu.SemaphoreType.DMA((len(cuts) + 1, groups)),
+            pltpu.SemaphoreType.DMA((len(cuts) + 1,)),
             pltpu.SemaphoreType.DMA((bits,)),
-            pltpu.SemaphoreType.DMA((len(units), bits)),
+            pltpu.SemaphoreType.DMA((max(slots_of(plan, bits).values()) + 1,)),
             pltpu.SemaphoreType.DMA,
             pltpu.SemaphoreType.DMA,
         ]
@@ -306,20 +345,19 @@
                 jax.ShapeDtypeStruct((steps, buckets), jnp.float32),
                 jax.ShapeDtypeStruct((1, columns), jnp.float32),
             ),
-            in_specs=[vmem, vmem, smem],
-            out_specs=(vmem, vmem, vmem),
+            in_specs=[vmem] * 4,
+            out_specs=(pl.BlockSpec(memory_space=pltpu.HBM),) * 3,
+            scratch_shapes=[pltpu.VMEM((steps, columns), jnp.bfloat16), pltpu.SemaphoreType.DMA((4,))],
             compiler_params=pltpu.CompilerParams(vmem_limit_bytes=8 * 1024 * 1024),
-        )(exact, peaks, bucket_of_row)
+        )(exact, last_row, peaks, scales)
         return unit.reshape(steps, 1, columns), peak_table, last
 
-    member = bucket_of_row[:, None] == jnp.arange(buckets, dtype=jnp.int32)[None, :]
-    by_bucket = jnp.max(jnp.where(member[:, :, None], peaks[:, None, :steps], 0.0), axis=0)
-    peak_table = lax.pmax(by_bucket.T, "tensor")
+    peak_table = lax.pmax(peaks, "tensor")
     own = lax.dynamic_slice_in_dim(bucket_of_row, lax.axis_index("dp"), 1, 0)
     own_member = own[:, None] == jnp.arange(buckets, dtype=jnp.int32)[None, :]
     own_peaks = jnp.max(jnp.where(own_member, peak_table, 0.0), axis=1, keepdims=True)
     unit = (exact / (own_peaks + epsilon)).astype(jnp.bfloat16)
-    return unit.reshape(steps, 1, columns), peak_table, exact[steps - 1 :]
+    return unit.reshape(steps, 1, columns), peak_table, last_row
 
 
 def solution(mesh):

time: 53 us -> 51.1 us (0.964)
  Pallas kernels: 52.2 us -> 50.3 us
    pallas_call x1, Pallas kernels: 50.8 us -> 49.5 us  [on_device(): pl.pallas_call(functools.partial(exchange, n, plan), out_shape=(jax.Shape...]
    pallas_call x1, Pallas kernels: 1.38 us -> 0.79 us  [on_device(): pl.pallas_call(finish, out_shape=(jax.ShapeDtypeStruct((steps, columns),...]
where the time goes in v3:
time: 51.1 us; the launch traced here: 50.9 us
  Pallas kernels  50.3 us (98%)
  between operations  0.64 us (1%)
    pallas_call x1, Pallas kernels, on_device(): pl.pallas_call(functools.partial(exchange, n, plan), out_shape=(jax.Shape...  49.5 us

profile of v3, /device:TPU:0, one launch (start us, length us, event | category | flops | bytes accessed | tf_op | source)
XLA Modules:
  0.0 50.9 jit_solution(9699322770468686632)
XLA Ops:
  0.6 49.5 %shard_map.76 = (f32[4,18432]{1,0:T(4,128)S(1)}, f32[1,18432]{1,0:T(1,128)S(1)}, f32[4,16]{1,0:T(4,128)S(1)}, f32[4,128]{1,0:T(4,128)S(1)}) custom-call(bf16[4,1,32,18432]{3,2,1,0:T(8,128)(2,1)} %codes.1, s32[4,1,16]{2,1,0:T(1,128)} %exponents_in.1, bf16[1,18432]{1,0:T(2,128)(2,1)} %accumulated_in.1, s32[32]{0:T(128)} %arrival_in.1, s32[32]{0:T(128)} %bucket_in.1), custom_call_target="tpu_custom_call" | custom-call | tf_op jit(solution)/shard_map/pallas_call | solution.py:305
  50.1 0.8 %shard_map.77 = (bf16[4,18432]{1,0:T(4,128)(2,1)}, f32[4,16]{1,0:T(4,128)}, f32[1,18432]{1,0:T(1,128)}) custom-call(f32[4,18432]{1,0:T(4,128)S(1)} %get-tuple-element.10.exact, f32[1,18432]{1,0:T(1,128)S(1)} %get-tuple-element.11.last_row, f32[4,16]{1,0:T(4,128)S(1)} %get-tuple-element.12.peaks, f32[4,128]{1,0:T(4,128)S(1)} %get-tuple-element.13.scales), custom_call_target="tpu_custom_call" | custom-call | tf_op jit(solution)/shard_map/pallas_call | solution.py:341

commit v4 on v3

--- a/solution.py
+++ b/solution.py
@@ -12,23 +12,24 @@
 VMEM_LIMIT = 48 * 1024 * 1024
 
 ORDERS = [
-    (0, 2, 3, 1, 4), (0, 2, 1, 3, 4), (0, 1, 3, 4, 2), (0, 3, 2, 1, 4),
+    (0, 1, 2, 3, 4), (0, 2, 3, 1, 4), (0, 3, 1, 2, 4), (0, 2, 1, 3, 4),
+    (0, 2, 3, 4, 1), (0, 3, 4, 1, 2), (0, 1, 3, 2, 4), (0, 3, 2, 4, 1),
     (0, 3, 4, 2, 1),
 ]
 UNITS = [
-    (0, 1, 0, 2, 4), (1, 1, 0, 2, 2), (1, 1, 2, 2, 1), (2, 1, 0, 4, 2), (3, 1, 0, 4, 4),
-    (4, 1, 0, 4, 1), (0, 1, 2, 2, 2), (5, 1, 0, 4, 1), (6, 1, 0, 4, 1), (7, 1, 0, 4, 2),
-    (8, 1, 0, 4, 1), (9, 1, 0, 4, 0), (10, 1, 0, 4, 2), (11, 1, 0, 2, 3), (12, 1, 0, 2, 3),
-    (13, 1, 0, 2, 1), (14, 1, 0, 4, 1), (13, 1, 2, 2, 1), (11, 1, 2, 2, 1), (15, 1, 0, 4, 2),
-    (16, 1, 0, 4, 2), (12, 1, 2, 2, 1), (17, 1, 0, 2, 1), (17, 1, 2, 2, 1),
+    (0, 1, 0, 2, 8), (1, 1, 0, 2, 4), (2, 1, 0, 4, 0), (3, 1, 0, 2, 7), (4, 1, 0, 4, 3),
+    (5, 1, 0, 2, 1), (6, 1, 0, 4, 8), (7, 1, 0, 4, 1), (0, 1, 2, 2, 8), (8, 1, 0, 4, 5),
+    (9, 1, 0, 4, 0), (10, 1, 0, 4, 0), (11, 1, 0, 4, 2), (12, 1, 0, 4, 0), (13, 1, 0, 4, 3),
+    (14, 1, 0, 4, 3), (1, 1, 2, 2, 3), (15, 1, 0, 4, 0), (3, 1, 2, 2, 0), (5, 1, 2, 2, 0),
+    (16, 1, 0, 4, 3), (17, 1, 0, 4, 6),
 ]
 TURNS = [
-    0, 1, 2, 3, 4, 5, 0, 1, 6, 2, 7, 8, 3, 9, 4, 5, 10, 6, 11, 7, 12, 8, 13, 9,
-    14, 0, 15, 10, 16, 1, 2, 11, 17, 18, 12, 19, 13, 14, 20, 15, 21, 16, 22, 17, 23, 18, 19, 3,
-    20, 21, 5, 22, 4, 23, 0, 1, 6, 13, 7, 9, 2, 14, 8, 4, 1, 3, 12, 6, 10, 9, 2, 19,
-    3, 11, 6, 12, 15, 20, 9, 2, 19, 5, 16, 7, 11, 12, 17, 8, 19, 18, 20, 10, 5, 15, 21, 7,
-    8, 16, 22, 11, 10, 17, 20, 23, 15, 0, 18, 5, 13, 21, 7, 16, 14, 22, 8, 17, 4, 23, 1, 11,
-    0, 3, 18, 6, 13, 10, 21, 9, 15, 12, 14, 19, 22, 20, 4, 23, 16, 17, 13, 18, 21, 14, 22, 23,
+    0, 1, 2, 3, 4, 0, 1, 5, 6, 2, 7, 3, 8, 9, 4, 10, 11, 6, 12, 10, 13, 7, 14, 15,
+    8, 13, 16, 1, 16, 17, 4, 18, 9, 19, 15, 12, 6, 20, 10, 3, 11, 18, 21, 16, 0, 20, 4, 13,
+    15, 9, 10, 11, 21, 14, 7, 3, 17, 8, 15, 20, 16, 19, 12, 18, 5, 10, 13, 2, 4, 21, 15, 11,
+    14, 18, 16, 17, 13, 7, 20, 5, 21, 1, 3, 11, 19, 15, 2, 12, 6, 18, 8, 17, 9, 0, 20, 14,
+    21, 5, 7, 19, 2, 12, 17, 5, 20, 10, 14, 0, 19, 1, 6, 9, 8, 16, 1, 21, 13, 9, 3, 18,
+    2, 4, 12, 14, 6, 7, 11, 8, 17, 0, 5, 19,
 ]
 CUTS = (2, 6)
 

time: 51.1 us -> 50.6 us (level)
  no operation moved by 1% of the time
where the time goes in v4:
time: 50.6 us; the launch traced here: 50.4 us
  Pallas kernels  49.8 us (98%)
  between operations  0.64 us (1%)
    pallas_call x1, Pallas kernels, on_device(): pl.pallas_call(functools.partial(exchange, n, plan), out_shape=(jax.Shape...  49 us

profile of v4, /device:TPU:0, one launch (start us, length us, event | category | flops | bytes accessed | tf_op | source)
XLA Modules:
  0.0 50.4 jit_solution(9364459525589467943)
XLA Ops:
  0.6 49.0 %shard_map.76 = (f32[4,18432]{1,0:T(4,128)S(1)}, f32[1,18432]{1,0:T(1,128)S(1)}, f32[4,16]{1,0:T(4,128)S(1)}, f32[4,128]{1,0:T(4,128)S(1)}) custom-call(bf16[4,1,32,18432]{3,2,1,0:T(8,128)(2,1)} %codes.1, s32[4,1,16]{2,1,0:T(1,128)} %exponents_in.1, bf16[1,18432]{1,0:T(2,128)(2,1)} %accumulated_in.1, s32[32]{0:T(128)} %arrival_in.1, s32[32]{0:T(128)} %bucket_in.1), custom_call_target="tpu_custom_call" | custom-call | tf_op jit(solution)/shard_map/pallas_call | solution.py:306
  49.7 0.8 %shard_map.77 = (bf16[4,18432]{1,0:T(4,128)(2,1)}, f32[4,16]{1,0:T(4,128)}, f32[1,18432]{1,0:T(1,128)}) custom-call(f32[4,18432]{1,0:T(4,128)S(1)} %get-tuple-element.10.exact, f32[1,18432]{1,0:T(1,128)S(1)} %get-tuple-element.11.last_row, f32[4,16]{1,0:T(4,128)S(1)} %get-tuple-element.12.peaks, f32[4,128]{1,0:T(4,128)S(1)} %get-tuple-element.13.scales), custom_call_target="tpu_custom_call" | custom-call | tf_op jit(solution)/shard_map/pallas_call | solution.py:342

commit v5 on v4

--- a/solution.py
+++ b/solution.py
@@ -13,23 +13,23 @@
 
 ORDERS = [
     (0, 1, 2, 3, 4), (0, 2, 3, 1, 4), (0, 3, 1, 2, 4), (0, 2, 1, 3, 4),
-    (0, 2, 3, 4, 1), (0, 3, 4, 1, 2), (0, 1, 3, 2, 4), (0, 3, 2, 4, 1),
+    (0, 2, 3, 4, 1), (0, 1, 3, 4, 2), (0, 3, 1, 4, 2), (0, 3, 4, 1, 2),
     (0, 3, 4, 2, 1),
 ]
 UNITS = [
-    (0, 1, 0, 2, 8), (1, 1, 0, 2, 4), (2, 1, 0, 4, 0), (3, 1, 0, 2, 7), (4, 1, 0, 4, 3),
-    (5, 1, 0, 2, 1), (6, 1, 0, 4, 8), (7, 1, 0, 4, 1), (0, 1, 2, 2, 8), (8, 1, 0, 4, 5),
-    (9, 1, 0, 4, 0), (10, 1, 0, 4, 0), (11, 1, 0, 4, 2), (12, 1, 0, 4, 0), (13, 1, 0, 4, 3),
-    (14, 1, 0, 4, 3), (1, 1, 2, 2, 3), (15, 1, 0, 4, 0), (3, 1, 2, 2, 0), (5, 1, 2, 2, 0),
-    (16, 1, 0, 4, 3), (17, 1, 0, 4, 6),
+    (0, 1, 0, 2, 7), (1, 1, 0, 2, 4), (1, 1, 2, 2, 5), (2, 1, 0, 2, 3), (3, 1, 0, 4, 3),
+    (2, 1, 2, 2, 6), (4, 1, 0, 2, 5), (5, 1, 0, 4, 8), (6, 1, 0, 4, 0), (7, 1, 0, 4, 8),
+    (8, 1, 0, 2, 2), (4, 1, 2, 2, 4), (9, 1, 0, 4, 1), (10, 1, 0, 4, 3), (11, 1, 0, 2, 1),
+    (12, 1, 0, 4, 0), (13, 1, 0, 4, 0), (14, 1, 0, 4, 3), (8, 1, 2, 2, 1), (15, 1, 0, 4, 5),
+    (16, 1, 0, 4, 0), (11, 1, 2, 2, 0), (17, 1, 0, 4, 3), (0, 1, 2, 2, 0),
 ]
 TURNS = [
-    0, 1, 2, 3, 4, 0, 1, 5, 6, 2, 7, 3, 8, 9, 4, 10, 11, 6, 12, 10, 13, 7, 14, 15,
-    8, 13, 16, 1, 16, 17, 4, 18, 9, 19, 15, 12, 6, 20, 10, 3, 11, 18, 21, 16, 0, 20, 4, 13,
-    15, 9, 10, 11, 21, 14, 7, 3, 17, 8, 15, 20, 16, 19, 12, 18, 5, 10, 13, 2, 4, 21, 15, 11,
-    14, 18, 16, 17, 13, 7, 20, 5, 21, 1, 3, 11, 19, 15, 2, 12, 6, 18, 8, 17, 9, 0, 20, 14,
-    21, 5, 7, 19, 2, 12, 17, 5, 20, 10, 14, 0, 19, 1, 6, 9, 8, 16, 1, 21, 13, 9, 3, 18,
-    2, 4, 12, 14, 6, 7, 11, 8, 17, 0, 5, 19,
+    0, 1, 2, 3, 4, 5, 0, 6, 1, 2, 7, 8, 5, 6, 3, 9, 4, 10, 7, 11, 12, 13, 14, 8,
+    15, 9, 11, 16, 3, 17, 13, 18, 19, 16, 0, 2, 10, 18, 6, 14, 7, 20, 21, 5, 11, 8, 12, 17,
+    1, 21, 22, 19, 18, 16, 5, 4, 13, 14, 22, 20, 9, 8, 3, 4, 6, 21, 15, 11, 13, 19, 3, 8,
+    2, 1, 23, 17, 12, 13, 23, 14, 20, 16, 10, 3, 18, 15, 19, 22, 17, 21, 7, 1, 12, 4, 23, 14,
+    20, 8, 16, 10, 0, 18, 15, 17, 22, 6, 5, 13, 23, 21, 12, 11, 9, 10, 19, 20, 15, 22, 5, 23,
+    9, 6, 7, 11, 0, 14, 2, 21, 10, 18, 17, 19, 1, 16, 2, 0, 9, 20, 12, 22, 4, 15, 7, 23,
 ]
 CUTS = (2, 6)
 

time: 50.6 us -> 50.7 us (level)
  no operation moved by 1% of the time
where the time goes in v5:
time: 50.7 us; the launch traced here: 50.5 us
  Pallas kernels  49.9 us (98%)
  between operations  0.64 us (1%)
    pallas_call x1, Pallas kernels, on_device(): pl.pallas_call(functools.partial(exchange, n, plan), out_shape=(jax.Shape...  49.1 us

profile of v5, /device:TPU:0, one launch (start us, length us, event | category | flops | bytes accessed | tf_op | source)
XLA Modules:
  0.0 50.5 jit_solution(17298626331513009992)
XLA Ops:
  0.6 49.1 %shard_map.76 = (f32[4,18432]{1,0:T(4,128)S(1)}, f32[1,18432]{1,0:T(1,128)S(1)}, f32[4,16]{1,0:T(4,128)S(1)}, f32[4,128]{1,0:T(4,128)S(1)}) custom-call(bf16[4,1,32,18432]{3,2,1,0:T(8,128)(2,1)} %codes.1, s32[4,1,16]{2,1,0:T(1,128)} %exponents_in.1, bf16[1,18432]{1,0:T(2,128)(2,1)} %accumulated_in.1, s32[32]{0:T(128)} %arrival_in.1, s32[32]{0:T(128)} %bucket_in.1), custom_call_target="tpu_custom_call" | custom-call | tf_op jit(solution)/shard_map/pallas_call | solution.py:306
  49.7 0.8 %shard_map.77 = (bf16[4,18432]{1,0:T(4,128)(2,1)}, f32[4,16]{1,0:T(4,128)}, f32[1,18432]{1,0:T(1,128)}) custom-call(f32[4,18432]{1,0:T(4,128)S(1)} %get-tuple-element.10.exact, f32[1,18432]{1,0:T(1,128)S(1)} %get-tuple-element.11.last_row, f32[4,16]{1,0:T(4,128)S(1)} %get-tuple-element.12.peaks, f32[4,128]{1,0:T(4,128)S(1)} %get-tuple-element.13.scales), custom_call_target="tpu_custom_call" | custom-call | tf_op jit(solution)/shard_map/pallas_call | solution.py:342
